TPU v7x, 32 devices: a whole 2x2x4 slice. The times are simulated.
32 devices in a mesh: shard: 2 (over core), ctx: 4 (over y, x), tp: 4 (over z).
Axes of the slice: x: 2, y: 2, z: 4, core: 2. Of those that a mesh axis runs over, the one named last changes fastest.
Arguments:
- layer_input: bfloat16 [8, 1024, 2048], P('shard', 'ctx'), may hold values from -6 to 6
- output_gradient: bfloat16 [8, 1024, 2048], P('shard', 'ctx'), may hold values from -6 to 6
- picture_piece_starts: int32 [8, 2], P('shard'), may hold values from 0 to 768, as said below
- sequence_adapter_index: int32 [8], P('shard'), may hold values from 0 to 7
- attention_norm_gain: float32 [2048], replicated, may hold values from 0.5 to 1.5
- attention_norm_bias: float32 [2048], replicated, may hold values from -1 to 1
- feedforward_norm_gain: float32 [2048], replicated, may hold values from 0.5 to 1.5
- feedforward_norm_bias: float32 [2048], replicated, may hold values from -1 to 1
- query_key_value_weight: bfloat16 [2048, 3, 2048], P('shard', None, 'tp'), may hold values from -0.125 to 0.125
- attention_output_weight: bfloat16 [2048, 2048], P('tp', 'shard'), may hold values from -0.375 to 0.375
- up_projection_weight: bfloat16 [2048, 8192], P('shard', 'tp'), may hold values from -0.125 to 0.125
- down_projection_weight: bfloat16 [8192, 2048], P('tp', 'shard'), may hold values from -0.09375 to 0.09375
- adapter_projection_first: bfloat16 [8, 2048, 16], replicated, may hold values from -0.125 to 0.125
- adapter_projection_second: bfloat16 [8, 16, 3, 2048], P(None, None, None, 'tp'), may hold values from -0.75 to 0.75
- adapter_heads_first: bfloat16 [8, 2048, 16], P(None, 'tp'), may hold values from -0.375 to 0.375
- adapter_heads_second: bfloat16 [8, 16, 2048], replicated, may hold values from -0.75 to 0.75
- adapter_up_first: bfloat16 [8, 2048, 16], replicated, may hold values from -0.125 to 0.125
- adapter_up_second: bfloat16 [8, 16, 8192], P(None, None, 'tp'), may hold values from -0.75 to 0.75
- adapter_down_first: bfloat16 [8, 8192, 16], P(None, 'tp'), may hold values from -0.09375 to 0.09375
- adapter_down_second: bfloat16 [8, 16, 2048], replicated, may hold values from -0.75 to 0.75
Outputs:
- layer_out: bfloat16 [8, 1024, 2048], P('shard', 'ctx')
- input_grad: bfloat16 [8, 1024, 2048], P('shard', 'ctx')
- qkv_in_grad: float32 [8, 2048, 16], replicated
- qkv_out_grad: float32 [8, 16, 3, 2048], P(None, None, None, 'tp')
- heads_in_grad: float32 [8, 2048, 16], P(None, 'tp')
- heads_out_grad: float32 [8, 16, 2048], replicated
- up_in_grad: float32 [8, 2048, 16], replicated
- up_out_grad: float32 [8, 16, 8192], P(None, None, 'tp')
- down_in_grad: float32 [8, 8192, 16], P(None, 'tp')
- down_out_grad: float32 [8, 16, 2048], replicated
Inputs may be any that keep to these rules, and one draw needn't show every extreme that they name: `picture_piece_starts`: piece c of a sequence starts within positions c * 512 to (c + 1) * 512 - 256, so pieces never meet; in some sequence a piece starts at 0, in some sequence a piece ends at 1024.
All inputs are finite; a program needn't handle non-finite values.
Results may differ from a plain program's by a relative error of at most 0.019.
Values may be sent and summed in bfloat16 or wider, within the bound.
A program may use at most 320 MiB of HBM per device.

v0:
```python
import jax
import jax.numpy as jnp
from jax import lax
from jax.sharding import PartitionSpec as P

HD = 128
PIC = 256
NORM_EPS = 1e-05


def layer_norm(inputs, gains, biases):
    average = jnp.mean(inputs, axis=-1, keepdims=True)
    centred = inputs - average
    spread = jnp.mean(centred * centred, axis=-1, keepdims=True)
    return centred * lax.rsqrt(spread + NORM_EPS) * gains + biases


def gelu_tanh(inputs):
    return (
        0.5
        * inputs
        * (1.0 + jnp.tanh(0.7978845608028654 * (inputs + 0.044715 * inputs * inputs * inputs)))
    )


def flattened_first(adapter_mat):
    adapter_tables, inner_dim, rank_width = adapter_mat.shape
    return jnp.transpose(adapter_mat, (1, 0, 2)).reshape(inner_dim, adapter_tables * rank_width)


def flattened_second(adapter_mat):
    return adapter_mat.reshape(adapter_mat.shape[0] * adapter_mat.shape[1], -1)


def unflat_in(grad_flat, adapter_tables):
    inner_dim = grad_flat.shape[0]
    return jnp.transpose(grad_flat.reshape(inner_dim, adapter_tables, -1), (1, 0, 2))


def matmul(left_mat, right_mat):
    return jnp.dot(left_mat, right_mat, preferred_element_type=jnp.float32)


def matmul_tn(left_mat, right_mat):
    return lax.dot_general(
        left_mat, right_mat, (((0,), (0,)), ((), ())), preferred_element_type=jnp.float32
    )


def matmul_nt(left_mat, right_mat):
    return lax.dot_general(
        left_mat, right_mat, (((1,), (1,)), ((), ())), preferred_element_type=jnp.float32
    )


def piece_labels(starts, positions):
    inside = (positions[None, None, :] >= starts[:, :, None]) & (
        positions[None, None, :] < starts[:, :, None] + PIC
    )
    labels = jnp.arange(1, starts.shape[1] + 1, dtype=jnp.int32)
    return jnp.sum(jnp.where(inside, labels[None, :, None], 0), axis=1)


def visible(query_pos, key_pos, query_labels, key_labels):
    causal = key_pos[None, None, :] <= query_pos[None, :, None]
    shared = (query_labels[:, :, None] == key_labels[:, None, :]) & (query_labels[:, :, None] > 0)
    return causal | shared


def exponents(queries, key_rows, query_pos, key_pos, visible_mask, slopes):
    score_scale = queries.shape[-1] ** (-0.5)
    logits = (
        jnp.einsum("sqhd,skhd->shqk", queries, key_rows, preferred_element_type=jnp.float32)
        * score_scale
    )
    distance = jnp.abs(query_pos[:, None] - key_pos[None, :]).astype(jnp.float32)
    logits = logits - slopes[None, :, None, None] * distance[None, None]
    return jnp.where(visible_mask[:, None], jnp.exp(logits), 0.0)


def block_grads(
    queries, scaled_grad, row_delta, key_rows, value_rows, query_pos, key_pos, visible_mask, slopes
):
    score_scale = queries.shape[-1] ** (-0.5)
    exponent = exponents(queries, key_rows, query_pos, key_pos, visible_mask, slopes)
    products_gv = jnp.einsum(
        "sqhd,skhd->shqk", scaled_grad, value_rows, preferred_element_type=jnp.float32
    )
    grad_logits = (
        exponent * (products_gv - jnp.transpose(row_delta, (0, 2, 1))[..., None])
    ).astype(jnp.bfloat16)
    grad_queries = (
        jnp.einsum("shqk,skhd->sqhd", grad_logits, key_rows, preferred_element_type=jnp.float32)
        * score_scale
    )
    grad_keyrows = (
        jnp.einsum("shqk,sqhd->skhd", grad_logits, queries, preferred_element_type=jnp.float32)
        * score_scale
    )
    grad_valrows = jnp.einsum(
        "shqk,sqhd->skhd",
        exponent.astype(jnp.bfloat16),
        scaled_grad,
        preferred_element_type=jnp.float32,
    )
    return (grad_queries, grad_keyrows, grad_valrows)


def tp_rows(rows_array, tp_count):
    chunk = rows_array.shape[0] // tp_count
    return lax.dynamic_slice_in_dim(rows_array, lax.axis_index("tp") * chunk, chunk, axis=0)


def scatter_rows(partials):
    widths = [part.shape[1] for part in partials]
    joined = lax.psum_scatter(
        jnp.concatenate(partials, axis=1), "tp", scatter_dimension=0, tiled=True
    )
    return split_columns(joined, widths)


def gather_rows(rows_here):
    widths = [part.shape[1] for part in rows_here]
    joined = lax.all_gather(jnp.concatenate(rows_here, axis=1), "tp", axis=0, tiled=True)
    return split_columns(joined, widths)


def split_columns(joined, widths):
    parts, offset = ([], 0)
    for width in widths:
        parts.append(joined[:, offset : offset + width])
        offset += width
    return tuple(parts)


def body(
    layer_input,
    output_gradient,
    picture_piece_starts,
    sequence_adapter_index,
    attention_norm_gain,
    attention_norm_bias,
    feedforward_norm_gain,
    feedforward_norm_bias,
    query_key_value_weight,
    attention_output_weight,
    up_projection_weight,
    down_projection_weight,
    adapter_projection_first,
    adapter_projection_second,
    adapter_heads_first,
    adapter_heads_second,
    adapter_up_first,
    adapter_up_second,
    adapter_down_first,
    adapter_down_second,
):
    seq_here, local_len, model_width = layer_input.shape
    tok_rows = seq_here * local_len
    tp_count = lax.axis_size("tp")
    adapter_tables = adapter_projection_first.shape[0]
    rank_width = adapter_projection_first.shape[2]
    head_width = HD
    device_heads = adapter_projection_second.shape[-1] // head_width
    local_width = device_heads * head_width
    columns = jnp.arange(adapter_tables * rank_width, dtype=jnp.int32) // rank_width
    chosen = (sequence_adapter_index[:, None] == columns[None, :]).astype(jnp.float32)
    select = jnp.broadcast_to(
        chosen[:, None, :], (seq_here, local_len, adapter_tables * rank_width)
    ).reshape(tok_rows, adapter_tables * rank_width)
    select_here = tp_rows(select, tp_count)
    head_ids = lax.axis_index("tp") * device_heads + jnp.arange(device_heads, dtype=jnp.int32)
    slopes = jnp.exp2(-8.0 * (head_ids.astype(jnp.float32) + 1.0) / (device_heads * tp_count))
    here_pos = lax.axis_index("ctx") * local_len + jnp.arange(local_len, dtype=jnp.int32)
    here_labels = piece_labels(picture_piece_starts, here_pos)
    heads_full = lax.all_gather(
        lax.all_gather(attention_output_weight, "tp", axis=0, tiled=True),
        "shard",
        axis=1,
        tiled=True,
    )
    heads_first_all = lax.all_gather(adapter_heads_first, "tp", axis=1, tiled=True)
    projection_first_flattened = flattened_first(adapter_projection_first)
    projection_second_flattened = flattened_second(adapter_projection_second)
    heads_first_flattened = flattened_first(adapter_heads_first)
    heads_first_all_flattened = flattened_first(heads_first_all)
    heads_second_flattened = flattened_second(adapter_heads_second)
    up_first_flattened = flattened_first(adapter_up_first)
    up_second_flattened = flattened_second(adapter_up_second)
    down_first_flattened = flattened_first(adapter_down_first)
    down_second_flattened = flattened_second(adapter_down_second)
    residual = layer_input.reshape(tok_rows, model_width).astype(jnp.float32)
    residual_here = tp_rows(residual, tp_count)
    first_norm = layer_norm(residual, attention_norm_gain, attention_norm_bias)
    first_act = first_norm.astype(jnp.bfloat16)
    _, first_back_full = jax.vjp(
        lambda inputs: layer_norm(inputs, attention_norm_gain, attention_norm_bias), residual_here
    )
    gathered_rows = (
        lax.all_gather(query_key_value_weight, "shard", axis=0, tiled=True),
        lax.all_gather(up_projection_weight, "shard", axis=0, tiled=True),
    )
    qkv_full = gathered_rows[0].reshape(model_width, 3 * local_width)
    up_full = gathered_rows[1]
    down_full = lax.all_gather(down_projection_weight, "shard", axis=1, tiled=True)
    first_low = (matmul(first_act, projection_first_flattened) * select).astype(jnp.bfloat16)
    projected = (
        matmul(first_act, qkv_full) + matmul(first_low, projection_second_flattened)
    ).astype(jnp.bfloat16)
    queries_flat = projected[:, :local_width].reshape(seq_here, local_len, local_width)
    queries = queries_flat.reshape(seq_here, local_len, device_heads, head_width)
    key_rows = projected[:, local_width : 2 * local_width].reshape(seq_here, local_len, local_width)
    value_rows = projected[:, 2 * local_width :].reshape(seq_here, local_len, local_width)
    pieces = (
        lax.all_gather(key_rows, "ctx", axis=1, tiled=True),
        lax.all_gather(value_rows, "ctx", axis=1, tiled=True),
    )
    piece_len = pieces[0].shape[1]
    key_pos = jnp.arange(piece_len, dtype=jnp.int32)
    key_labels = piece_labels(picture_piece_starts, key_pos)
    visible_mask = visible(here_pos, key_pos, here_labels, key_labels)
    piece_keys = pieces[0].reshape(seq_here, piece_len, device_heads, head_width)
    piece_values = pieces[1].reshape(seq_here, piece_len, device_heads, head_width)
    exponent = exponents(queries, piece_keys, here_pos, key_pos, visible_mask, slopes)
    weighted = jnp.einsum(
        "shqk,skhd->sqhd",
        exponent.astype(jnp.bfloat16),
        piece_values,
        preferred_element_type=jnp.float32,
    )
    weighted, totals = (weighted, jnp.sum(exponent, axis=-1))
    per_total = jnp.transpose(totals, (0, 2, 1))[..., None]
    heads_raw = weighted / per_total
    heads_act = heads_raw.reshape(tok_rows, local_width).astype(jnp.bfloat16)
    heads_act_here = lax.all_to_all(heads_act, "tp", 0, 1, tiled=True)
    attn_here = matmul(heads_act_here, heads_full)
    heads_low_here = (matmul(heads_act_here, heads_first_all_flattened) * select_here).astype(
        jnp.bfloat16
    )
    middle_here = residual_here + attn_here + matmul(heads_low_here, heads_second_flattened)
    second_norm, second_back = jax.vjp(
        lambda inputs: layer_norm(inputs, feedforward_norm_gain, feedforward_norm_bias), middle_here
    )
    second_act_here = second_norm.astype(jnp.bfloat16)
    (second_act,) = gather_rows((second_act_here,))
    up_low = (matmul(second_act, up_first_flattened) * select).astype(jnp.bfloat16)
    hidden = matmul(second_act, up_full) + matmul(up_low, up_second_flattened)
    activated, gelu_back = jax.vjp(gelu_tanh, hidden)
    activated = activated.astype(jnp.bfloat16)
    down_part = matmul(activated, down_full)
    down_low_part = matmul(activated, down_first_flattened)
    ffn_here, ffn_low_here = scatter_rows((down_part, down_low_part))
    down_low_here = (ffn_low_here * select_here).astype(jnp.bfloat16)
    result_here = (middle_here + ffn_here + matmul(down_low_here, down_second_flattened)).astype(
        jnp.bfloat16
    )
    result_rows, down_low = gather_rows((result_here, down_low_here))
    layer_out = result_rows.reshape(layer_input.shape)
    grad_top_low = output_gradient.reshape(tok_rows, model_width)
    grad_top_here = tp_rows(grad_top_low, tp_count).astype(jnp.float32)
    down_back = (matmul_nt(grad_top_low, down_second_flattened) * select).astype(jnp.bfloat16)
    grad_down_in = matmul_tn(activated, down_back)
    grad_activated = matmul_nt(grad_top_low, down_full) + matmul_nt(down_back, down_first_flattened)
    grad_hidden = gelu_back(grad_activated)[0].astype(jnp.bfloat16)
    up_second_gradient = matmul_tn(up_low, grad_hidden)
    ffn_back_part = matmul_nt(grad_hidden, up_full)
    ffn_back_low = matmul_nt(grad_hidden, up_second_flattened)
    back_here, back_low_here = scatter_rows((ffn_back_part, ffn_back_low))
    up_back_here = (back_low_here * select_here).astype(jnp.bfloat16)
    grad_second = back_here + matmul_nt(up_back_here, up_first_flattened)
    grad_middle_here = grad_top_here + second_back(grad_second)[0]
    grad_middle_low_here = grad_middle_here.astype(jnp.bfloat16)
    heads_back_here = (
        matmul_nt(grad_middle_low_here, heads_second_flattened) * select_here
    ).astype(jnp.bfloat16)
    up_back, heads_back = gather_rows((up_back_here, heads_back_here))
    down_second_gradient = matmul_tn(down_low, grad_top_low)
    grad_up_in = matmul_tn(second_act, up_back)
    heads_second_gradient = matmul_tn(heads_low_here, grad_middle_low_here)
    grad_heads_in = matmul_tn(heads_act, heads_back)
    grad_heads_here = (
        matmul_nt(grad_middle_low_here, heads_full)
        + matmul_nt(heads_back_here, heads_first_all_flattened)
    ).astype(jnp.bfloat16)
    grad_heads = lax.all_to_all(grad_heads_here, "tp", 1, 0, tiled=True)
    grad_heads_wide = grad_heads.reshape(seq_here, local_len, device_heads, head_width).astype(
        jnp.float32
    )
    scaled_grad = (grad_heads_wide / per_total).astype(jnp.bfloat16)
    row_delta = jnp.sum(grad_heads_wide * heads_raw, axis=-1) / per_total[..., 0]
    grad_queries, grad_keyrows, grad_valrows = block_grads(
        queries,
        scaled_grad,
        row_delta,
        piece_keys,
        piece_values,
        here_pos,
        key_pos,
        visible_mask,
        slopes,
    )
    grad_keys_all, grad_values_all = (
        lax.psum_scatter(grad_keyrows, "ctx", scatter_dimension=1, tiled=True),
        lax.psum_scatter(grad_valrows, "ctx", scatter_dimension=1, tiled=True),
    )
    grad_projected = jnp.concatenate(
        [
            grad_queries.reshape(tok_rows, local_width),
            grad_keys_all.reshape(tok_rows, local_width),
            grad_values_all.reshape(tok_rows, local_width),
        ],
        axis=1,
    ).astype(jnp.bfloat16)
    projection_second_gradient = matmul_tn(first_low, grad_projected)
    attn_back_part = matmul_nt(grad_projected, qkv_full)
    attn_back_low = matmul_nt(grad_projected, projection_second_flattened)
    first_here, first_low_here = scatter_rows((attn_back_part, attn_back_low))
    qkv_back_here = (first_low_here * select_here).astype(jnp.bfloat16)
    grad_first = first_here + matmul_nt(qkv_back_here, projection_first_flattened)
    input_here = (grad_middle_here + first_back_full(grad_first)[0]).astype(jnp.bfloat16)
    input_rows, qkv_back = gather_rows((input_here, qkv_back_here))
    input_grad = input_rows.reshape(layer_input.shape)
    grad_qkv_in = matmul_tn(first_act, qkv_back)
    heads_second_total = lax.psum(heads_second_gradient, "tp")
    adapter_terms = (
        unflat_in(grad_qkv_in, adapter_tables),
        projection_second_gradient.reshape(adapter_projection_second.shape),
        unflat_in(grad_heads_in, adapter_tables),
        heads_second_total.reshape(adapter_heads_second.shape),
        unflat_in(grad_up_in, adapter_tables),
        up_second_gradient.reshape(adapter_up_second.shape),
        unflat_in(grad_down_in, adapter_tables),
        down_second_gradient.reshape(adapter_down_second.shape),
    )
    summed = lax.psum(adapter_terms, ("shard", "ctx"))
    return (
        layer_out,
        input_grad,
        summed[0],
        summed[1],
        summed[2],
        summed[3],
        summed[4],
        summed[5],
        summed[6],
        summed[7],
    )


def solution(mesh):
    placed = (
        P("shard", "ctx", None),
        P("shard", "ctx", None),
        P("shard", None),
        P("shard"),
        P(),
        P(),
        P(),
        P(),
        P("shard", None, "tp"),
        P("tp", "shard"),
        P("shard", "tp"),
        P("tp", "shard"),
        P(),
        P(None, None, None, "tp"),
        P(None, "tp", None),
        P(),
        P(),
        P(None, None, "tp"),
        P(None, "tp", None),
        P(),
    )
    return jax.shard_map(
        body,
        mesh=mesh,
        in_specs=placed,
        out_specs=(
            P("shard", "ctx", None),
            P("shard", "ctx", None),
            P(),
            P(None, None, None, "tp"),
            P(None, "tp", None),
            P(),
            P(),
            P(None, None, "tp"),
            P(None, "tp", None),
            P(),
        ),
        check_vma=False,
    )
```

profile of v0, /device:TPU:0, one launch (start us, length us, event | category | flops | bytes accessed | tf_op | source)
XLA Modules:
  0.0 1514.2 jit_solution(5506899695237392603)
XLA Ops:
  7.2 4.7 copy.75
  13.4 3.2 convert_reduce_fusion
  23.0 8.6 all-gather.11.cloned.1.call-done
  31.6 10.1 fusion.40
  45.4 69.8 %all-gather.17.cloned.1.call-done = bf16[2048,1024]{1,0:T(8,128)(2,1)} async-done(((bf16[512,1024]{1,0:T(8,128)(2,1)}), bf16[2048,1024]{1,0:T(8,128)(2,1)}) %all-gather.17.cloned.1.call-update) | async-done | bytes 4194320 | tf_op jit(solution)/shard_map/all_gather | solution.py:177
  117.2 2.6 broadcast_multiply_fusion
  123.6 45.1 %all-gather.13.cloned.1.call-done = bf16[4,1024,512]{2,1,0:T(8,128)(2,1)} async-done(((bf16[4,256,512]{2,1,0:T(8,128)(2,1)}), bf16[4,1024,512]{2,1,0:T(8,128)(2,1)}) %all-gather.13.cloned.1.call-update) | async-done | bytes 4194320 | tf_op jit(solution)/shard_map/all_gather | solution.py:216
  168.7 6.3 copy.77
  175.0 48.4 %all-gather.15.cloned.1.call-done = bf16[4,1024,512]{1,2,0:T(8,128)(2,1)} async-done(((bf16[4,256,512]{1,2,0:T(8,128)(2,1)}), bf16[4,1024,512]{1,2,0:T(8,128)(2,1)}) %all-gather.15.cloned.1.call-update) | async-done | bytes 4194320 | tf_op jit(solution)/shard_map/all_gather | solution.py:215
  223.4 14.3 fusion.37
  237.7 11.8 fusion.38
  249.5 4.6 all-to-all-start
  254.1 8.5 convert.22
  262.6 27.4 %all_gather.41 = bf16[8,2048,16]{1,2,0:T(8,128)(2,1)S(1)} all-gather(bf16[8,512,16]{1,2,0:T(8,128)(2,1)S(1)} %copy-done.44), channel_id=1, replica_groups=mesh['shard'=2,'ctx'=4,'tp'=4] {'tp'}, dimensions={1}, use_global_device_ids=true | all-gather | bytes 655360 | tf_op jit(solution)/shard_map/all_gather | solution.py:182
  290.6 6.4 convolution_add_fusion.6
  299.5 3.6 fusion.23
  303.1 14.9 fusion.44
  317.9 62.5 %all-gather.21.cloned.1.call-done = bf16[1024,2048]{1,0:T(8,128)(2,1)} async-done(((bf16[256,2048]{1,0:T(8,128)(2,1)}), bf16[1024,2048]{1,0:T(8,128)(2,1)}) %all-gather.21.cloned.1.call-update) | async-done | bytes 4194320 | tf_op jit(solution)/shard_map/all_gather | solution.py:124
  380.4 15.4 %fusion.41 = f32[1024,2048]{1,0:T(8,128)} fusion(bf16[1024,2048]{1,0:T(8,128)(2,1)} %all-gather.21.cloned.1.call-done, bf16[2048,2048]{1,0:T(8,128)(2,1)} %all-gather.23.cloned.1.call-done), kind=kOutput, calls=%fused_computation.122 | convolution fusion | flops 8589934592 | bytes 20971520 | tf_op jit(solution)/shard_map/dot_general | solution.py:41
  397.1 6.9 multiply_convert_fusion.1
  404.0 9.6 fusion.3
  415.7 8.9 fusion.45
  424.5 4.2 pad_maximum_fusion.1
  429.2 151.1 %reduce-scatter.8.cloned.1.call-done = f32[256,2176]{1,0:T(8,128)} async-done(((f32[1024,2176]{1,0:T(8,128)}), f32[256,2176]{1,0:T(8,128)}) %reduce-scatter.8.cloned.1.call-update) | async-done | bytes 2228240 | tf_op jit(solution)/shard_map/reduce_scatter | solution.py:116
  581.3 2.4 multiply_reduce_fusion.4
  587.9 2.4 fusion.47
  593.9 30.1 %all_to_all.29 = bf16[256,4,512]{0,2,1:T(8,128)(2,1)S(1)} all-to-all(bf16[256,4,512]{0,2,1:T(8,128)(2,1)} %bitcast.197), channel_id=1, replica_groups=mesh['shard'=2,'ctx'=4,'tp'=4] {'tp'}, dimensions={1} | all-to-all | bytes 2097152 | tf_op jit(solution)/shard_map/all_to_all | solution.py:285
  627.5 9.2 multiply_convert_fusion
  636.7 3.3 copy-done.2
  640.0 4.9 multiply_bitcast_fusion
  645.0 11.7 fusion.10
  656.9 3.8 fusion.43
  660.8 11.3 fusion.42
  672.1 4.2 pad_maximum_fusion
  676.4 9.0 fusion.19
  685.4 2.4 copy.87
  687.7 2.5 bitcast_dynamic-update-slice_fusion.2
  690.2 40.2 %reduce-scatter.10.cloned.1.call-done = f32[4,256,4,128]{1,3,2,0:T(8,128)} async-done(((f32[4,1024,4,128]{1,3,2,0:T(8,128)}), f32[4,256,4,128]{1,3,2,0:T(8,128)}) %reduce-scatter.10.cloned.1.call-update) | async-done | bytes 2097168 | tf_op jit(solution)/shard_map/reduce_scatter | solution.py:303
  730.4 2.7 convert.17
  733.1 2.3 copy.89
  735.5 84.4 %reduce-scatter.12.cloned.1.call-done = f32[4,256,4,128]{1,3,2,0:T(8,128)} async-done(((f32[4,1024,4,128]{1,3,2,0:T(8,128)}), f32[4,256,4,128]{1,3,2,0:T(8,128)}) %reduce-scatter.12.cloned.1.call-update) | async-done | bytes 2097168 | tf_op jit(solution)/shard_map/reduce_scatter | solution.py:304
  819.8 2.7 convert.18
  824.9 2.4 bitcast_dynamic-update-slice_fusion.1
  827.3 2.7 bitcast_dynamic-update-slice_fusion
  830.0 3.0 fusion.49
  833.0 8.8 fusion.48
  841.8 4.2 pad_maximum_fusion.2
  848.1 126.9 %reduce-scatter.6.cloned.1.call-done = f32[256,2176]{1,0:T(8,128)} async-done(((f32[1024,2176]{1,0:T(8,128)}), f32[256,2176]{1,0:T(8,128)}) %reduce-scatter.6.cloned.1.call-update) | async-done | bytes 2228240 | tf_op jit(solution)/shard_map/reduce_scatter | solution.py:116
  975.0 156.1 %reduce-scatter.14.cloned.1.call-done = f32[256,2176]{1,0:T(8,128)} async-done(((f32[1024,2176]{1,0:T(8,128)}), f32[256,2176]{1,0:T(8,128)}) %reduce-scatter.14.cloned.1.call-update) | async-done | bytes 2228240 | tf_op jit(solution)/shard_map/reduce_scatter | solution.py:116
  1132.1 3.0 multiply_reduce_fusion.2
  1135.1 2.4 fusion.34
  1145.9 4.2 fusion.52
  1151.9 24.1 %all_gather.47 = bf16[1024,256]{1,0:T(8,128)(2,1)S(1)} all-gather(bf16[256,256]{1,0:T(8,128)(2,1)S(1)} %pad_maximum_fusion.5), channel_id=1, replica_groups=mesh['shard'=2,'ctx'=4,'tp'=4] {'tp'}, dimensions={0}, use_global_device_ids=true | all-gather | bytes 655360 | tf_op jit(solution)/shard_map/all_gather | solution.py:124
  1178.5 3.9 fusion.26
  1182.4 2.5 fusion.50
  1186.5 48.3 %all-gather.29.cloned.1.call-done = bf16[1024,2176]{1,0:T(8,128)(2,1)} async-done(((bf16[256,2176]{1,0:T(8,128)(2,1)}), bf16[1024,2176]{1,0:T(8,128)(2,1)}) %all-gather.29.cloned.1.call-update) | async-done | bytes 4456464 | tf_op jit(solution)/shard_map/all_gather | solution.py:124
  1235.8 84.0 %all-gather.27.cloned.1.call-done = bf16[1024,2176]{1,0:T(8,128)(2,1)} async-done(((bf16[256,2176]{1,0:T(8,128)(2,1)}), bf16[1024,2176]{1,0:T(8,128)(2,1)}) %all-gather.27.cloned.1.call-update) | async-done | bytes 4456464 | tf_op jit(solution)/shard_map/all_gather | solution.py:124
  1321.1 4.0 fusion.54
  1326.8 46.1 %all-reduce.4.cloned.1.call-done = f32[8,16,2048]{2,1,0:T(8,128)} async-done(((f32[8,16,2048]{2,1,0:T(8,128)}), f32[8,16,2048]{2,1,0:T(8,128)}) %all-reduce.4.cloned.1.call-update) | async-done | bytes 1048592 | tf_op jit(solution)/shard_map/psum | solution.py:324
  1373.0 4.9 slice.65
  1377.9 2.6 slice.70
  1380.5 115.5 %all-reduce.6.cloned.1.call-done = (f32[8,2048,16]{1,2,0:T(8,128)}, f32[8,16,3,512]{3,2,1,0:T(4,128)}, f32[8,512,16]{1,2,0:T(8,128)}, f32[8,16,2048]{2,1,0:T(8,1...) async-done(((f32[8,2048,16]{1,2,0:T(8,128)}, f32[8,16,3,512]{3,2,1,0:T(4,128)}, ...) | async-done | bytes 7340048 | tf_op jit(solution)/shard_map/psum | solution.py:335
  1496.0 2.5 copy.96
  1498.5 2.4 copy.123
  (234 shorter events, 66.4 us)
Async XLA Ops:
  7.2 389.8 %copy-start = (bf16[8,16,2048]{2,1,0:T(8,128)(2,1)S(1)}, bf16[8,16,2048]{2,1,0:T(8,128)(2,1)}, u32[]{:S(2)}) copy-start(bf16[8,16,2048]{2,1,0:T(8,128)(2,1)} %param.37) | copy-start | bytes 1572868
  7.2 5.6 copy-start.43
  7.2 24.4 %all-gather.11.cloned.1.call-start = ((), (), s32[]{:S(2)}) async-start(), calls=%async_computation.7 | async-start | bytes 9437184 | tf_op jit(solution)/shard_map/all_gather | solution.py:200
  12.0 103.2 %all-gather.17.cloned.1.call-start = ((), (), s32[]{:S(2)}) async-start(), calls=%async_computation.10 | async-start | bytes 5242880 | tf_op jit(solution)/shard_map/all_gather | solution.py:177
  12.8 155.9 %all-gather.13.cloned.1.call-start = ((), (), s32[]{:S(2)}) async-start(), calls=%async_computation.8 | async-start | bytes 5242880 | tf_op jit(solution)/shard_map/all_gather | solution.py:216
  12.8 3.8 copy-start.3
  13.3 28.4 %copy-start.20 = (bf16[16,8,3,512]{3,1,2,0:T(8,128)(2,1)}, bf16[16,8,3,512]{3,1,2,0:T(8,128)(2,1)S(1)}, u32[]{:S(2)}) copy-start(bf16[16,8,3,512]{3,1,2,0:T(8,128)(2,1)S(1)} %copy.105) | copy-start | bytes 1179652
  13.4 4.5 copy-start.46
  13.4 4.5 copy-start.51
  17.9 3.8 copy-start.26
  23.0 18.7 %copy-start.22 = (bf16[1024,128]{1,0:T(8,128)(2,1)}, bf16[1024,128]{1,0:T(8,128)(2,1)S(1)}, u32[]{:S(2)}) copy-start(bf16[1024,128]{1,0:T(8,128)(2,1)S(1)} %fusion.21) | copy-start | bytes 786436
  44.0 179.4 %all-gather.15.cloned.1.call-start = ((), (), s32[]{:S(2)}) async-start(), calls=%async_computation.9 | async-start | bytes 5242880 | tf_op jit(solution)/shard_map/all_gather | solution.py:215
  45.3 245.2 %all-gather.19.cloned.1.call-start = ((), (), s32[]{:S(2)}) async-start(), calls=%async_computation.11 | async-start | bytes 12582912 | tf_op jit(solution)/shard_map/all_gather | solution.py:176
  115.2 187.9 %all-gather.25.cloned.1.call-start = ((), (), s32[]{:S(2)}) async-start(), calls=%async_computation.14 | async-start | bytes 12582912 | tf_op jit(solution)/shard_map/all_gather | solution.py:205
  115.8 202.1 %all-gather.23.cloned.1.call-start = ((), (), s32[]{:S(2)}) async-start(), calls=%async_computation.13 | async-start | bytes 12582912 | tf_op jit(solution)/shard_map/all_gather | solution.py:201
  123.6 99.8 %copy-start.14 = (bf16[4,256,4,128]{1,3,2,0:T(8,128)(2,1)}, bf16[4,256,4,128]{1,3,2,0:T(8,128)(2,1)S(1)}, u32[]{:S(2)}) copy-start(bf16[4,256,4,128]{1,3,2,0:T(8,128)(2,1)S(1)} %copy.88) | copy-start | bytes 3145732
  223.4 14.3 copy-start.4
  249.5 40.5 %all-to-all-start = ((bf16[4,256,512]{1,2,0:T(8,128)(2,1)}), bf16[4,256,512]{1,2,0:T(8,128)(2,1)S(1)}, u32[]{:S(2)}, u32[]{:S(2)}) async-start(bf16[4,256,512]{1,2,0:T(8,128)(2,1)} %bitcast.12), calls=%async_computation | async-start | bytes 2097152 | tf_op jit(solution)/shard_map/all_to_all | solution.py:235
  254.1 126.2 %all-gather.21.cloned.1.call-start = ((), (), s32[]{:S(2)}) async-start(), calls=%async_computation.12 | async-start | bytes 5242880 | tf_op jit(solution)/shard_map/all_gather | solution.py:124
  254.1 8.5 copy-start.44
  290.1 6.9 copy-start.18
  290.6 6.5 copy-start.40
  290.6 6.5 copy-start.29
  299.4 281.0 %reduce-scatter.8.cloned.1.call-start = ((), (), s32[]{:S(2)}) async-start(), calls=%async_computation.17 | async-start | bytes 11141120 | tf_op jit(solution)/shard_map/reduce_scatter | solution.py:116
  380.4 15.4 %copy-start.6 = (bf16[1024,2048]{1,0:T(8,128)(2,1)S(1)}, bf16[1024,2048]{1,0:T(8,128)(2,1)}, u32[]{:S(2)}) copy-start(bf16[1024,2048]{1,0:T(8,128)(2,1)} %all-gather.21.cloned.1.call-done) | copy-start | bytes 12582916
  380.4 15.4 %copy-start.24 = (bf16[8,2048,16]{1,2,0:T(8,128)(2,1)S(1)}, bf16[8,2048,16]{1,2,0:T(8,128)(2,1)}, u32[]{:S(2)}) copy-start(bf16[8,2048,16]{1,2,0:T(8,128)(2,1)} %param.36) | copy-start | bytes 1572868
  397.0 7.0 copy-start.31
  397.0 6.9 copy-start.42
  397.0 18.6 %slice-start.4 = ((s8[8388608]{0:T(1024)(128)(4,1)}), s8[4194304]{0:T(1024)(128)(4,1)S(1)}, s32[]{:S(2)}) async-start(s8[8388608]{0:T(1024)(128)(4,1)} %bitcast.221), calls=%async_computation.28 | async-start | bytes 8388608
  404.0 11.7 slice-start.5
  428.8 152.5 %copy-start.25 = (bf16[8,2048,16]{1,2,0:T(8,128)(2,1)S(1)}, bf16[8,2048,16]{1,2,0:T(8,128)(2,1)}, u32[]{:S(2)}) copy-start(bf16[8,2048,16]{1,2,0:T(8,128)(2,1)} %param.36) | copy-start | bytes 1572868
  428.8 301.6 %reduce-scatter.10.cloned.1.call-start = ((), (), s32[]{:S(2)}) async-start(), calls=%async_computation.18 | async-start | bytes 10485760 | tf_op jit(solution)/shard_map/reduce_scatter | solution.py:303
  581.3 6.5 slice-start
  583.7 3.7 copy-start.30
  583.7 4.2 slice-start.1
  627.5 12.5 copy-start.15
  636.7 3.3 copy-start.2
  644.9 174.9 %reduce-scatter.12.cloned.1.call-start = ((), (), s32[]{:S(2)}) async-start(), calls=%async_computation.19 | async-start | bytes 10485760 | tf_op jit(solution)/shard_map/reduce_scatter | solution.py:304
  656.7 318.3 %reduce-scatter.6.cloned.1.call-start = ((), (), s32[]{:S(2)}) async-start(), calls=%async_computation.15 | async-start | bytes 11141120 | tf_op jit(solution)/shard_map/reduce_scatter | solution.py:116
  656.9 3.9 copy-start.7
  676.3 454.7 %reduce-scatter.14.cloned.1.call-start = ((), (), s32[]{:S(2)}) async-start(), calls=%async_computation.20 | async-start | bytes 11141120 | tf_op jit(solution)/shard_map/reduce_scatter | solution.py:116
  735.5 94.5 %copy-start.21 = (bf16[16,8,3,512]{3,1,2,0:T(8,128)(2,1)S(1)}, bf16[16,8,3,512]{3,1,2,0:T(8,128)(2,1)}, u32[]{:S(2)}) copy-start(bf16[16,8,3,512]{3,1,2,0:T(8,128)(2,1)} %copy-done.20) | copy-start | bytes 1179652
  830.0 3.0 copy-start.5
  846.0 286.1 %copy-start.27 = (bf16[8,2048,16]{1,2,0:T(8,128)(2,1)S(1)}, bf16[8,2048,16]{1,2,0:T(8,128)(2,1)}, u32[]{:S(2)}) copy-start(bf16[8,2048,16]{1,2,0:T(8,128)(2,1)} %param.32) | copy-start | bytes 1572868
  846.0 286.1 %copy-start.47 = (f32[2048]{0:T(1024)S(1)}, f32[2048]{0:T(1024)}, u32[]{:S(2)}) copy-start(f32[2048]{0:T(1024)} %param.24) | copy-start | bytes 24580
  846.0 388.8 %all-gather.29.cloned.1.call-start = ((), (), s32[]{:S(2)}) async-start(), calls=%async_computation.21 | async-start | bytes 5570560 | tf_op jit(solution)/shard_map/all_gather | solution.py:124
  1137.5 3.0 copy-start.28
  1140.5 179.3 %all-gather.27.cloned.1.call-start = ((), (), s32[]{:S(2)}) async-start(), calls=%async_computation.16 | async-start | bytes 5570560 | tf_op jit(solution)/shard_map/all_gather | solution.py:124
  1142.6 3.3 copy-start.32
  1143.7 229.2 %all-reduce.4.cloned.1.call-start = ((), (), s32[]{:S(2)}) async-start(), calls=%async_computation.22 | async-start | bytes 2097152 | tf_op jit(solution)/shard_map/psum | solution.py:324
  1145.9 4.2 copy-start.8
  1151.8 25.3 %copy-start.17 = (bf16[256,2048]{1,0:T(8,128)(2,1)S(1)}, bf16[256,2048]{1,0:T(8,128)(2,1)}, u32[]{:S(2)}) copy-start(bf16[256,2048]{1,0:T(8,128)(2,1)} %copy-done.16) | copy-start | bytes 3145732
  1151.8 25.3 %copy-start.41 = (bf16[256,128]{1,0:T(8,128)(2,1)S(1)}, bf16[256,128]{1,0:T(8,128)(2,1)}, u32[]{:S(2)}) copy-start(bf16[256,128]{1,0:T(8,128)(2,1)} %copy-done.40) | copy-start | bytes 196612
  1177.1 5.3 copy-start.23
  1178.5 317.5 %all-reduce.6.cloned.1.call-start = ((), (), s32[]{:S(2)}) async-start(), calls=%async_computation.23 | async-start | bytes 15204352 | tf_op jit(solution)/shard_map/psum | solution.py:335
  1321.1 4.0 copy-start.10
  1372.9 5.0 slice-start.2
  1373.0 5.0 slice-start.3
  1496.0 6.6 copy-start.37
  1496.0 7.5 copy-start.36
  1496.0 8.5 copy-start.35
  1498.5 7.0 copy-start.34
  1502.6 3.9 copy-start.33
  1502.6 4.9 copy-start.1
  (14 other events, 25.7 us)
Sparse Core Ops, SparseCore 0:
  12.1 19.4 all-gather.10
  33.2 81.9 all-gather.16
  117.6 51.0 all-gather.12
  170.9 52.4 all-gather.14
  224.8 19.8 all-gather.18
  246.1 21.0 all-gather.24
  268.7 21.0 all-gather.22
  299.5 80.7 all-gather.20
  428.9 151.4 reduce-scatter.7
  645.0 85.3 reduce-scatter.9
  733.5 86.3 reduce-scatter.11
  822.1 152.8 reduce-scatter.5
  977.3 153.7 reduce-scatter.13
  1140.6 94.1 all-gather.28
  1236.2 83.5 all-gather.26
  1322.6 50.3 all-reduce.3
  1378.1 117.8 all-reduce.5
where the time goes:
time: 1520 us; the launch traced here: 1510 us
  waiting for transfers between devices  1090 us (72%)
  matrix products  201 us (13%)
  blocking collectives  81.7 us (5%)
  local copies, waits for them, and re-layouts  66.4 us (4%)
  other arithmetic  54.7 us (4%)
    reduce_scatter x3, waiting for transfers between devices, scatter_rows(): lax.psum_scatter(jnp.concatenate(partials, axis=1), 'tp', scatter_dimensi...  434 us
    all_gather x3, waiting for transfers between devices, gather_rows(): lax.all_gather(jnp.concatenate(rows_here, axis=1), 'tp', axis=0, tiled=True)  195 us
    psum x1, waiting for transfers between devices, body(): summed = lax.psum(adapter_terms, ('shard', 'ctx'))  115 us
    reduce_scatter x1, waiting for transfers between devices, body(): lax.psum_scatter(grad_valrows, 'ctx', scatter_dimension=1, tiled=True)  84.4 us
    all_gather x1, waiting for transfers between devices, body(): lax.all_gather(attention_output_weight, 'tp', axis=0, tiled=True)  69.8 us
    dot_general x12, matrix products, matmul(): return jnp.dot(left_mat, right_mat, preferred_element_type=jnp.float32)  60.3 us
    dot_general x12, matrix products, matmul_nt(): lax.dot_general(left_mat, right_mat, (((1,), (1,)), ((), ())), preferred_...  59.5 us
    all_gather x1, waiting for transfers between devices, body(): lax.all_gather(key_rows, 'ctx', axis=1, tiled=True)  48.4 us
  transfers between devices with their start and end apart: 18, of which 14 were waited for; matrix products, arithmetic and copies ran while one was open for 14% of the time, Pallas kernels for 0%

commit v1 on v0

--- a/solution.py
+++ b/solution.py
@@ -6,6 +6,15 @@
 HD = 128
 PIC = 256
 NORM_EPS = 1e-05
+
+
+def add_in_pairs(value, mesh_axis):
+    size = lax.axis_size(mesh_axis)
+    total, hop = (value, 1)
+    while hop < size:
+        total = total + lax.ppermute(total, mesh_axis, [(i, i ^ hop) for i in range(size)])
+        hop = 2 * hop
+    return total
 
 
 def layer_norm(inputs, gains, biases):
@@ -321,7 +330,7 @@
     input_rows, qkv_back = gather_rows((input_here, qkv_back_here))
     input_grad = input_rows.reshape(layer_input.shape)
     grad_qkv_in = matmul_tn(first_act, qkv_back)
-    heads_second_total = lax.psum(heads_second_gradient, "tp")
+    heads_second_total = add_in_pairs(heads_second_gradient, "tp")
     adapter_terms = (
         unflat_in(grad_qkv_in, adapter_tables),
         projection_second_gradient.reshape(adapter_projection_second.shape),

time: 1520 us -> 1510 us (level)
  waiting for transfers between devices: 1090 us -> 994 us
  blocking collectives: 81.7 us -> 158 us
    all_gather x3, waiting for transfers between devices: 195 us -> 86.7 us  [gather_rows(): lax.all_gather(jnp.concatenate(rows_here, axis=1), 'tp', axis=0, tiled=True)]
    all_gather x1, blocking collectives: 24.1 us -> 100 us  [gather_rows(): lax.all_gather(jnp.concatenate(rows_here, axis=1), 'tp', axis=0, tiled=True)]
    ppermute x0 -> x2, waiting for transfers between devices: none -> 66.2 us  [add_in_pairs(): lax.ppermute(total, mesh_axis, [(i, i ^ hop) for i in range(size)])]
    psum x1 -> x0, waiting for transfers between devices: 46.1 us -> none  [body(): heads_second_total = lax.psum(heads_second_gradient, 'tp')]
  transfers between devices with their start and end apart: 18 -> 19, of which waited for: 14 -> 13; matrix products, arithmetic and copies ran while one was open for 14% -> 14% of each run, Pallas kernels for 0% -> 0%
where the time goes in v1:
time: 1510 us; the launch traced here: 1500 us
  waiting for transfers between devices  994 us (66%)
  matrix products  199 us (13%)
  blocking collectives  158 us (10%)
  local copies, waits for them, and re-layouts  68 us (5%)
  other arithmetic  57.1 us (4%)
  between operations  15.1 us (1%)
    reduce_scatter x3, waiting for transfers between devices, scatter_rows(): lax.psum_scatter(jnp.concatenate(partials, axis=1), 'tp', scatter_dimensi...  434 us
    psum x1, waiting for transfers between devices, body(): summed = lax.psum(adapter_terms, ('shard', 'ctx'))  109 us
    all_gather x1, blocking collectives, gather_rows(): lax.all_gather(jnp.concatenate(rows_here, axis=1), 'tp', axis=0, tiled=True)  100 us
    all_gather x3, waiting for transfers between devices, gather_rows(): lax.all_gather(jnp.concatenate(rows_here, axis=1), 'tp', axis=0, tiled=True)  86.7 us
    reduce_scatter x1, waiting for transfers between devices, body(): lax.psum_scatter(grad_valrows, 'ctx', scatter_dimension=1, tiled=True)  84.4 us
    all_gather x1, waiting for transfers between devices, body(): lax.all_gather(attention_output_weight, 'tp', axis=0, tiled=True)  69.8 us
    ppermute x2, waiting for transfers between devices, add_in_pairs(): lax.ppermute(total, mesh_axis, [(i, i ^ hop) for i in range(size)])  66.2 us
    dot_general x12, matrix products, matmul(): return jnp.dot(left_mat, right_mat, preferred_element_type=jnp.float32)  60.4 us
  transfers between devices with their start and end apart: 19, of which 13 were waited for; matrix products, arithmetic and copies ran while one was open for 14% of the time, Pallas kernels for 0%

profile of v1, /device:TPU:0, one launch (start us, length us, event | category | flops | bytes accessed | tf_op | source)
XLA Modules:
  0.0 1503.5 jit_solution(6230461259534484888)
XLA Ops:
  7.2 4.7 copy.75
  13.4 3.2 convert_reduce_fusion
  23.0 8.6 all-gather.11.cloned.1.call-done
  31.6 10.1 fusion.40
  45.4 69.8 %all-gather.17.cloned.1.call-done = bf16[2048,1024]{1,0:T(8,128)(2,1)} async-done(((bf16[512,1024]{1,0:T(8,128)(2,1)}), bf16[2048,1024]{1,0:T(8,128)(2,1)}) %all-gather.17.cloned.1.call-update) | async-done | bytes 4194320 | tf_op jit(solution)/shard_map/all_gather | solution.py:186
  117.2 2.6 broadcast_multiply_fusion
  123.6 45.1 %all-gather.13.cloned.1.call-done = bf16[4,1024,512]{2,1,0:T(8,128)(2,1)} async-done(((bf16[4,256,512]{2,1,0:T(8,128)(2,1)}), bf16[4,1024,512]{2,1,0:T(8,128)(2,1)}) %all-gather.13.cloned.1.call-update) | async-done | bytes 4194320 | tf_op jit(solution)/shard_map/all_gather | solution.py:225
  168.7 6.3 copy.77
  175.0 48.4 %all-gather.15.cloned.1.call-done = bf16[4,1024,512]{1,2,0:T(8,128)(2,1)} async-done(((bf16[4,256,512]{1,2,0:T(8,128)(2,1)}), bf16[4,1024,512]{1,2,0:T(8,128)(2,1)}) %all-gather.15.cloned.1.call-update) | async-done | bytes 4194320 | tf_op jit(solution)/shard_map/all_gather | solution.py:224
  223.4 14.3 fusion.37
  237.7 11.8 fusion.38
  249.5 4.6 all-to-all-start
  254.1 8.5 convert.22
  262.6 27.4 %all_gather.41 = bf16[8,2048,16]{1,2,0:T(8,128)(2,1)S(1)} all-gather(bf16[8,512,16]{1,2,0:T(8,128)(2,1)S(1)} %copy-done.45), channel_id=1, replica_groups=mesh['shard'=2,'ctx'=4,'tp'=4] {'tp'}, dimensions={1}, use_global_device_ids=true | all-gather | bytes 655360 | tf_op jit(solution)/shard_map/all_gather | solution.py:191
  290.6 6.4 convolution_add_fusion.6
  299.5 3.6 fusion.23
  303.1 15.1 %fusion.44 = f32[1024,2048]{1,0:T(8,128)} fusion(bf16[1024,2048]{1,0:T(8,128)(2,1)} %bitcast.164, bf16[2048,2048]{1,0:T(8,128)(2,1)} %all-gather.25.cloned.1.call-done), kind=kOutput, calls=%fused_computation.125 | convolution fusion | flops 8589934592 | bytes 20971520 | tf_op jit(solution)/shard_map/dot_general | solution.py:60
  318.1 62.3 %all-gather.21.cloned.1.call-done = bf16[1024,2048]{1,0:T(8,128)(2,1)} async-done(((bf16[256,2048]{1,0:T(8,128)(2,1)}), bf16[1024,2048]{1,0:T(8,128)(2,1)}) %all-gather.21.cloned.1.call-update) | async-done | bytes 4194320 | tf_op jit(solution)/shard_map/all_gather | solution.py:133
  380.4 15.5 %fusion.41 = f32[1024,2048]{1,0:T(8,128)} fusion(bf16[1024,2048]{1,0:T(8,128)(2,1)} %all-gather.21.cloned.1.call-done, bf16[2048,2048]{1,0:T(8,128)(2,1)} %all-gather.23.cloned.1.call-done), kind=kOutput, calls=%fused_computation.122 | convolution fusion | flops 8589934592 | bytes 20971520 | tf_op jit(solution)/shard_map/dot_general | solution.py:50
  397.2 6.9 multiply_convert_fusion.1
  404.1 9.6 fusion.3
  415.8 8.9 fusion.45
  424.7 4.2 pad_maximum_fusion.1
  429.3 151.1 %reduce-scatter.8.cloned.1.call-done = f32[256,2176]{1,0:T(8,128)} async-done(((f32[1024,2176]{1,0:T(8,128)}), f32[256,2176]{1,0:T(8,128)}) %reduce-scatter.8.cloned.1.call-update) | async-done | bytes 2228240 | tf_op jit(solution)/shard_map/reduce_scatter | solution.py:125
  581.4 2.4 multiply_reduce_fusion.4
  588.0 2.4 fusion.47
  594.0 30.1 %all_to_all.29 = bf16[256,4,512]{0,2,1:T(8,128)(2,1)S(1)} all-to-all(bf16[256,4,512]{0,2,1:T(8,128)(2,1)} %bitcast.196), channel_id=1, replica_groups=mesh['shard'=2,'ctx'=4,'tp'=4] {'tp'}, dimensions={1} | all-to-all | bytes 2097152 | tf_op jit(solution)/shard_map/all_to_all | solution.py:294
  627.6 9.2 multiply_convert_fusion
  636.8 3.3 copy-done.2
  640.0 4.9 multiply_bitcast_fusion
  645.0 11.6 fusion.10
  656.9 3.8 fusion.43
  660.9 11.3 fusion.42
  672.1 4.2 pad_maximum_fusion
  676.4 9.0 fusion.19
  685.4 2.4 copy.87
  687.8 2.5 bitcast_dynamic-update-slice_fusion.2
  690.3 40.2 %reduce-scatter.10.cloned.1.call-done = f32[4,256,4,128]{1,3,2,0:T(8,128)} async-done(((f32[4,1024,4,128]{1,3,2,0:T(8,128)}), f32[4,256,4,128]{1,3,2,0:T(8,128)}) %reduce-scatter.10.cloned.1.call-update) | async-done | bytes 2097168 | tf_op jit(solution)/shard_map/reduce_scatter | solution.py:312
  730.5 2.7 convert.17
  733.2 2.3 copy.89
  735.5 84.4 %reduce-scatter.12.cloned.1.call-done = f32[4,256,4,128]{1,3,2,0:T(8,128)} async-done(((f32[4,1024,4,128]{1,3,2,0:T(8,128)}), f32[4,256,4,128]{1,3,2,0:T(8,128)}) %reduce-scatter.12.cloned.1.call-update) | async-done | bytes 2097168 | tf_op jit(solution)/shard_map/reduce_scatter | solution.py:313
  819.9 2.7 convert.18
  822.6 2.3 copy.90
  824.9 2.4 bitcast_dynamic-update-slice_fusion.1
  827.4 2.7 bitcast_dynamic-update-slice_fusion
  830.1 3.0 fusion.49
  833.1 8.8 fusion.48
  841.9 4.2 pad_maximum_fusion.2
  848.2 126.9 %reduce-scatter.6.cloned.1.call-done = f32[256,2176]{1,0:T(8,128)} async-done(((f32[1024,2176]{1,0:T(8,128)}), f32[256,2176]{1,0:T(8,128)}) %reduce-scatter.6.cloned.1.call-update) | async-done | bytes 2228240 | tf_op jit(solution)/shard_map/reduce_scatter | solution.py:125
  975.1 156.1 %reduce-scatter.14.cloned.1.call-done = f32[256,2176]{1,0:T(8,128)} async-done(((f32[1024,2176]{1,0:T(8,128)}), f32[256,2176]{1,0:T(8,128)}) %reduce-scatter.14.cloned.1.call-update) | async-done | bytes 2228240 | tf_op jit(solution)/shard_map/reduce_scatter | solution.py:125
  1132.2 3.0 multiply_reduce_fusion.2
  1135.2 2.4 fusion.34
  1149.6 4.3 fusion.52
  1155.7 66.2 %collective-permute-done = f32[128,2048]{1,0:T(8,128)} collective-permute-done((f32[128,2048]{1,0:T(8,128)S(1)}, f32[128,2048]{1,0:T(8,128)}, u32[]{:S(2)}, u32[]{:S(2)}) %collective-permute-start) | collective-permute-done | bytes 1048608 | tf_op jit(solution)/shard_map/ppermute | solution.py:15
  1223.2 4.7 collective-permute-start.1
  1227.8 100.4 %all_gather.47 = bf16[1024,256]{1,0:T(8,128)(2,1)S(1)} all-gather(bf16[256,256]{1,0:T(8,128)(2,1)S(1)} %pad_maximum_fusion.5), channel_id=1, replica_groups=mesh['shard'=2,'ctx'=4,'tp'=4] {'tp'}, dimensions={0}, use_global_device_ids=true | all-gather | bytes 655360 | tf_op jit(solution)/shard_map/all_gather | solution.py:133
  1328.5 2.4 convolution_bitcast_fusion.1
  1337.1 24.4 %all-gather.27.cloned.1.call-done = bf16[1024,2176]{1,0:T(8,128)(2,1)} async-done(((bf16[256,2176]{1,0:T(8,128)(2,1)}), bf16[1024,2176]{1,0:T(8,128)(2,1)}) %all-gather.27.cloned.1.call-update) | async-done | bytes 4456464 | tf_op jit(solution)/shard_map/all_gather | solution.py:133
  1362.6 4.0 convolution_bitcast_fusion
  1368.4 5.7 slice.65
  1374.1 2.6 slice.70
  1376.7 108.6 %all-reduce.3.cloned.1.call-done = (f32[8,2048,16]{1,2,0:T(8,128)}, f32[8,16,3,512]{3,2,1,0:T(4,128)}, f32[8,512,16]{1,2,0:T(8,128)}, f32[8,16,2048]{2,1,0:T(8,1...) async-done(((f32[8,2048,16]{1,2,0:T(8,128)}, f32[8,16,3,512]{3,2,1,0:T(4,128)}, ...) | async-done | bytes 7340048 | tf_op jit(solution)/shard_map/psum | solution.py:344
  1485.3 2.5 copy.96
  1487.8 2.4 copy.122
  (239 shorter events, 70.1 us)
Async XLA Ops:
  7.2 390.0 %copy-start = (bf16[8,16,2048]{2,1,0:T(8,128)(2,1)S(1)}, bf16[8,16,2048]{2,1,0:T(8,128)(2,1)}, u32[]{:S(2)}) copy-start(bf16[8,16,2048]{2,1,0:T(8,128)(2,1)} %param.37) | copy-start | bytes 1572868
  7.2 5.6 copy-start.44
  7.2 24.4 %all-gather.11.cloned.1.call-start = ((), (), s32[]{:S(2)}) async-start(), calls=%async_computation.7 | async-start | bytes 9437184 | tf_op jit(solution)/shard_map/all_gather | solution.py:209
  12.0 103.2 %all-gather.17.cloned.1.call-start = ((), (), s32[]{:S(2)}) async-start(), calls=%async_computation.10 | async-start | bytes 5242880 | tf_op jit(solution)/shard_map/all_gather | solution.py:186
  12.8 155.9 %all-gather.13.cloned.1.call-start = ((), (), s32[]{:S(2)}) async-start(), calls=%async_computation.8 | async-start | bytes 5242880 | tf_op jit(solution)/shard_map/all_gather | solution.py:225
  12.8 3.8 copy-start.3
  13.3 28.4 %copy-start.21 = (bf16[16,8,3,512]{3,1,2,0:T(8,128)(2,1)}, bf16[16,8,3,512]{3,1,2,0:T(8,128)(2,1)S(1)}, u32[]{:S(2)}) copy-start(bf16[16,8,3,512]{3,1,2,0:T(8,128)(2,1)S(1)} %copy.105) | copy-start | bytes 1179652
  13.4 4.5 copy-start.47
  13.4 4.5 copy-start.52
  17.9 3.8 copy-start.27
  23.0 18.7 %copy-start.23 = (bf16[1024,128]{1,0:T(8,128)(2,1)}, bf16[1024,128]{1,0:T(8,128)(2,1)S(1)}, u32[]{:S(2)}) copy-start(bf16[1024,128]{1,0:T(8,128)(2,1)S(1)} %fusion.21) | copy-start | bytes 786436
  44.0 179.4 %all-gather.15.cloned.1.call-start = ((), (), s32[]{:S(2)}) async-start(), calls=%async_computation.9 | async-start | bytes 5242880 | tf_op jit(solution)/shard_map/all_gather | solution.py:224
  45.3 245.2 %all-gather.19.cloned.1.call-start = ((), (), s32[]{:S(2)}) async-start(), calls=%async_computation.11 | async-start | bytes 12582912 | tf_op jit(solution)/shard_map/all_gather | solution.py:185
  115.2 187.9 %all-gather.25.cloned.1.call-start = ((), (), s32[]{:S(2)}) async-start(), calls=%async_computation.14 | async-start | bytes 12582912 | tf_op jit(solution)/shard_map/all_gather | solution.py:214
  115.8 202.4 %all-gather.23.cloned.1.call-start = ((), (), s32[]{:S(2)}) async-start(), calls=%async_computation.13 | async-start | bytes 12582912 | tf_op jit(solution)/shard_map/all_gather | solution.py:210
  123.6 99.8 %copy-start.16 = (bf16[4,256,4,128]{1,3,2,0:T(8,128)(2,1)}, bf16[4,256,4,128]{1,3,2,0:T(8,128)(2,1)S(1)}, u32[]{:S(2)}) copy-start(bf16[4,256,4,128]{1,3,2,0:T(8,128)(2,1)S(1)} %copy.88) | copy-start | bytes 3145732
  223.4 14.3 copy-start.4
  249.5 40.5 %all-to-all-start = ((bf16[4,256,512]{1,2,0:T(8,128)(2,1)}), bf16[4,256,512]{1,2,0:T(8,128)(2,1)S(1)}, u32[]{:S(2)}, u32[]{:S(2)}) async-start(bf16[4,256,512]{1,2,0:T(8,128)(2,1)} %bitcast.12), calls=%async_computation | async-start | bytes 2097152 | tf_op jit(solution)/shard_map/all_to_all | solution.py:244
  254.1 126.2 %all-gather.21.cloned.1.call-start = ((), (), s32[]{:S(2)}) async-start(), calls=%async_computation.12 | async-start | bytes 5242880 | tf_op jit(solution)/shard_map/all_gather | solution.py:133
  254.1 8.5 copy-start.45
  290.1 6.9 copy-start.19
  290.6 6.5 copy-start.41
  290.6 6.5 copy-start.30
  299.4 281.0 %reduce-scatter.8.cloned.1.call-start = ((), (), s32[]{:S(2)}) async-start(), calls=%async_computation.17 | async-start | bytes 11141120 | tf_op jit(solution)/shard_map/reduce_scatter | solution.py:125
  380.4 15.5 %copy-start.8 = (bf16[1024,2048]{1,0:T(8,128)(2,1)S(1)}, bf16[1024,2048]{1,0:T(8,128)(2,1)}, u32[]{:S(2)}) copy-start(bf16[1024,2048]{1,0:T(8,128)(2,1)} %all-gather.21.cloned.1.call-done) | copy-start | bytes 12582916
  380.4 15.5 %copy-start.25 = (bf16[8,2048,16]{1,2,0:T(8,128)(2,1)S(1)}, bf16[8,2048,16]{1,2,0:T(8,128)(2,1)}, u32[]{:S(2)}) copy-start(bf16[8,2048,16]{1,2,0:T(8,128)(2,1)} %param.36) | copy-start | bytes 1572868
  397.1 7.0 copy-start.32
  397.1 7.0 copy-start.43
  397.2 18.6 %slice-start.4 = ((s8[8388608]{0:T(1024)(128)(4,1)}), s8[4194304]{0:T(1024)(128)(4,1)S(1)}, s32[]{:S(2)}) async-start(s8[8388608]{0:T(1024)(128)(4,1)} %bitcast.221), calls=%async_computation.27 | async-start | bytes 8388608
  404.1 11.7 slice-start.5
  428.9 152.5 %copy-start.26 = (bf16[8,2048,16]{1,2,0:T(8,128)(2,1)S(1)}, bf16[8,2048,16]{1,2,0:T(8,128)(2,1)}, u32[]{:S(2)}) copy-start(bf16[8,2048,16]{1,2,0:T(8,128)(2,1)} %param.36) | copy-start | bytes 1572868
  428.9 301.6 %reduce-scatter.10.cloned.1.call-start = ((), (), s32[]{:S(2)}) async-start(), calls=%async_computation.18 | async-start | bytes 10485760 | tf_op jit(solution)/shard_map/reduce_scatter | solution.py:312
  581.4 6.5 slice-start
  583.7 3.7 copy-start.31
  583.8 4.2 slice-start.1
  587.4 2.9 copy-start.18
  627.6 12.5 copy-start.17
  636.8 3.3 copy-start.2
  645.0 174.9 %reduce-scatter.12.cloned.1.call-start = ((), (), s32[]{:S(2)}) async-start(), calls=%async_computation.19 | async-start | bytes 10485760 | tf_op jit(solution)/shard_map/reduce_scatter | solution.py:313
  656.7 318.4 %reduce-scatter.6.cloned.1.call-start = ((), (), s32[]{:S(2)}) async-start(), calls=%async_computation.15 | async-start | bytes 11141120 | tf_op jit(solution)/shard_map/reduce_scatter | solution.py:125
  656.9 3.9 copy-start.10
  676.4 454.8 %reduce-scatter.14.cloned.1.call-start = ((), (), s32[]{:S(2)}) async-start(), calls=%async_computation.20 | async-start | bytes 11141120 | tf_op jit(solution)/shard_map/reduce_scatter | solution.py:125
  735.5 94.5 %copy-start.22 = (bf16[16,8,3,512]{3,1,2,0:T(8,128)(2,1)S(1)}, bf16[16,8,3,512]{3,1,2,0:T(8,128)(2,1)}, u32[]{:S(2)}) copy-start(bf16[16,8,3,512]{3,1,2,0:T(8,128)(2,1)} %copy-done.21) | copy-start | bytes 1179652
  830.1 3.0 copy-start.6
  846.1 286.0 %copy-start.28 = (bf16[8,2048,16]{1,2,0:T(8,128)(2,1)S(1)}, bf16[8,2048,16]{1,2,0:T(8,128)(2,1)}, u32[]{:S(2)}) copy-start(bf16[8,2048,16]{1,2,0:T(8,128)(2,1)} %param.32) | copy-start | bytes 1572868
  846.1 286.0 %copy-start.48 = (f32[2048]{0:T(1024)S(1)}, f32[2048]{0:T(1024)}, u32[]{:S(2)}) copy-start(f32[2048]{0:T(1024)} %param.24) | copy-start | bytes 24580
  846.1 489.8 %all-gather.29.cloned.1.call-start = ((), (), s32[]{:S(2)}) async-start(), calls=%async_computation.21 | async-start | bytes 5570560 | tf_op jit(solution)/shard_map/all_gather | solution.py:133
  1137.6 3.0 copy-start.29
  1140.5 221.0 %all-gather.27.cloned.1.call-start = ((), (), s32[]{:S(2)}) async-start(), calls=%async_computation.16 | async-start | bytes 5570560 | tf_op jit(solution)/shard_map/all_gather | solution.py:133
  1140.6 3.2 copy-start.42
  1143.7 5.8 copy-start.33
  1143.8 341.5 %all-reduce.3.cloned.1.call-start = ((), (), s32[]{:S(2)}) async-start(), calls=%async_computation.22 | async-start | bytes 15204352 | tf_op jit(solution)/shard_map/psum | solution.py:344
  1145.4 76.4 %collective-permute-start = (f32[128,2048]{1,0:T(8,128)S(1)}, f32[128,2048]{1,0:T(8,128)}, u32[]{:S(2)}, u32[]{:S(2)}) collective-permute-start(f32[128,2048]{1,0:T(8,128)S(1)} %fusion.51), channel_id=1, source_target_pairs={{0,1},{1,0},{2,3},{3,2},{4,5},{5,4},{6,7},{7,6},{8,9},{9,8},{10,11... | collective-permute-start | bytes 3145736 | tf_op jit(solution)/shard_map/ppermute | solution.py:15
  1149.6 4.4 copy-start.11
  1223.2 109.5 %collective-permute-start.1 = (f32[128,2048]{1,0:T(8,128)S(1)}, f32[128,2048]{1,0:T(8,128)S(1)}, u32[]{:S(2)}, u32[]{:S(2)}) collective-permute-start(f32[128,2048]{1,0:T(8,128)S(1)} %add.215), channel_id=1, source_target_pairs={{0,2},{1,3},{2,0},{3,1},{4,6},{5,7},{6,4},{7,5},{8,10},{9,11},{10,... | collective-permute-start | bytes 3145736 | tf_op jit(solution)/shard_map/ppermute | solution.py:15
  1362.6 4.0 copy-start.5
  1368.4 5.7 slice-start.2
  1368.4 5.7 slice-start.3
  1485.3 6.6 copy-start.38
  1485.3 7.5 copy-start.37
  1485.3 8.5 copy-start.36
  1487.8 7.0 copy-start.35
  1491.8 3.9 copy-start.34
  1491.8 4.9 copy-start.1
  (16 other events, 30.9 us)
Sparse Core Ops, SparseCore 0:
  12.1 19.4 all-gather.10
  33.2 81.9 all-gather.16
  117.6 51.0 all-gather.12
  170.9 52.4 all-gather.14
  224.8 19.8 all-gather.18
  246.1 21.0 all-gather.24
  268.7 21.0 all-gather.22
  299.5 80.7 all-gather.20
  429.0 151.3 reduce-scatter.7
  645.1 85.3 reduce-scatter.9
  733.6 86.3 reduce-scatter.11
  822.1 152.8 reduce-scatter.5
  977.4 153.6 reduce-scatter.13
  1140.7 116.5 all-gather.28
  1258.6 102.8 all-gather.26
  1368.5 116.7 all-reduce.2
